TPU v7x, 32 devices: a whole 2x2x4 slice. The times are simulated.
32 devices in a mesh: lon: 4 (over z), lat: 4 (over x, core), mem: 2 (over y).
Axes of the slice: x: 2, y: 2, z: 4, core: 2. Of those that a mesh axis runs over, the one named last changes fastest.
Arguments:
- tokens: bfloat16 [4, 8, 136, 24, 192], P('mem', None, 'lat', 'lon'), parts along dimension 0, may hold values from -6 to 6
- band_rows: int32 [4, 2], P('lat'), may hold values from 0 to 89, as said below
- down_gain: float32 [768], replicated, may hold values from 0.1 to 1.9
- down_shift: float32 [768], replicated, may hold values from -3 to 3
- down_weight: bfloat16 [768, 384], P(('lon', 'lat')), may hold values from -0.21875 to 0.21875
- up_weight: bfloat16 [384, 768], P(('lon', 'lat')), may hold values from -0.3125 to 0.3125
- up_gain: float32 [192], replicated, may hold values from 0.1 to 1.9
- up_shift: float32 [192], replicated, may hold values from -3 to 3
- mix_weight: bfloat16 [192, 192], replicated, may hold values from -0.4375 to 0.4375
Outputs:
- expanded: bfloat16 [4, 8, 136, 24, 192], P('mem', None, 'lat', 'lon'), parts along dimension 0
There are 2 independent parts, one for each index of `mem`. A program takes and returns all parts, laid end to end along the dimension named above; an argument that names none is the same for every part. Nothing has to cross between parts.
Inputs may be any that keep to these rules, and one draw needn't show every extreme that they name: `band_rows`: row b holds band b's first latitude row and one past its last; the bands cover rows 0 to 88 in order without gaps; band 0 holds an odd number of rows and every other band an even number; each band holds at least 2 * (5) rows and at most 34, and some band other than band 0 holds exactly 34.
All inputs are finite; a program needn't handle non-finite values.
Results may differ from a plain program's by a relative error of at most 0.0062.
Values may be sent and summed in bfloat16 or wider, within the bound.
No kernel may reach another device: no remote copies, remote signals or barrier semaphores. Data moves between devices by JAX's collectives and lax.ppermute only.
A program may use at most 64 MiB of HBM per device.

v0:
```python
import jax
import jax.numpy as jnp
from jax import lax
from jax.experimental import pallas as pl
from jax.experimental.pallas import tpu as pltpu
from jax.sharding import PartitionSpec as P


EPS = 1e-05
LANES = 128
PAD = 64
F32 = jnp.float32
BF16 = jnp.bfloat16
VMEM = pl.BlockSpec(memory_space=pltpu.VMEM)
SMEM = pl.BlockSpec(memory_space=pltpu.SMEM)
HBM = pl.BlockSpec(memory_space=pltpu.HBM)
ORDER = ((0, 0), (0, 1), (1, 0), (1, 1))


def passed_along(block, axis, distance):
    devices = range(lax.axis_size(axis))
    route = [(i, i + distance) for i in devices if i + distance in devices]
    return lax.ppermute(block, axis, route)


def swapped(block, axis, partner):
    n = lax.axis_size(axis)
    return lax.ppermute(block, axis, [(i, partner(i)) for i in range(n)])


def band(band_ref):
    odd = lax.rem(band_ref[0, 0], 2)
    return odd, band_ref[0, 1] - band_ref[0, 0]


def room(mebibytes):
    return pltpu.CompilerParams(vmem_limit_bytes=mebibytes * 2**20)


def cost(flops, moved):
    return pl.CostEstimate(flops=flops, bytes_accessed=moved, transcendentals=0)


def centred(weight, features):
    blocks = []
    for start in range(0, weight.shape[-1], features):
        block = weight[..., start : start + features].astype(F32)
        blocks.append(block - jnp.mean(block, axis=-1, keepdims=True))
    return jnp.concatenate(blocks, axis=-1).astype(BF16)


def joined(pair):
    return jnp.concatenate([pair[0].astype(F32), pair[1].astype(F32)], axis=-1).astype(BF16)


def first_kernel(
    band_ref, tokens_ref, down_ref, up_ref, shard_ref, core_ref, across_ref, down_s, up_s, rows, sem
):
    tiles, up_tiles = down_ref.shape[0], up_ref.shape[0]
    half, features = up_ref.shape[2] // 2, tokens_ref.shape[4]
    _, live = band(band_ref)
    even = lax.rem(lax.axis_index("lat"), 2) == 0
    last = live - 1
    sources = [
        (down_ref, down_s),
        (up_ref, up_s),
        (tokens_ref.at[:, jnp.where(even, last, 0)], rows.at[0]),
        (tokens_ref.at[:, jnp.where(even, 0, last)], rows.at[1]),
    ]
    copies = [pltpu.make_async_copy(*pair, sem.at[i]) for i, pair in enumerate(sources)]
    for copy in copies:
        copy.start()
    copies[0].wait()
    copies[1].wait()
    up = centred(up_s[...], features)
    for ref in (shard_ref, core_ref, across_ref):
        ref[:tiles] = down_s[...]
        ref[tiles : tiles + up_tiles] = up[..., :half]
        ref[tiles + up_tiles : tiles + 2 * up_tiles] = up[..., half:]
    for side, ref in enumerate((core_ref, across_ref)):
        copies[2 + side].wait()
        ref[tiles + 2 * up_tiles :] = joined(rows[side])


def first_sends(band_rows, tokens, down, up):
    members, _, columns, levels, features = tokens.shape
    tiles, up_tiles = down.shape[0] // 8, up.shape[0] // 8
    n, wide = tiles + 2 * up_tiles, down.shape[1]
    shard = jax.ShapeDtypeStruct((n, 8, wide), BF16)
    with_row = jax.ShapeDtypeStruct((n + columns, 8, wide), BF16)
    return pl.pallas_call(
        first_kernel,
        out_shape=(shard, with_row, with_row),
        in_specs=[SMEM, HBM, HBM, HBM],
        out_specs=(VMEM,) * 3,
        scratch_shapes=[
            pltpu.VMEM((tiles, 8, wide), BF16),
            pltpu.VMEM((up_tiles, 8, up.shape[1]), BF16),
            pltpu.VMEM((2, members, columns, levels, features), BF16),
            pltpu.SemaphoreType.DMA((4,)),
        ],
        compiler_params=room(2),
        name="first",
    )(band_rows, tokens, down.reshape(tiles, 8, -1), up.reshape(up_tiles, 8, -1))


def rows_kernel(band_ref, tokens_ref, first_ref, last_ref, rows, sem):
    _, live = band(band_ref)
    copies = [
        pltpu.make_async_copy(tokens_ref.at[:, row], rows.at[i], sem.at[i])
        for i, row in enumerate((0, live - 1))
    ]
    for copy in copies:
        copy.start()
    for side, out_ref in enumerate((first_ref, last_ref)):
        copies[side].wait()
        out_ref[...] = joined(rows[side])


def rows_of(band_rows, tokens):
    members, _, columns, levels, features = tokens.shape
    row = jax.ShapeDtypeStruct((columns, levels, members * features), BF16)
    return pl.pallas_call(
        rows_kernel,
        out_shape=(row, row),
        in_specs=[SMEM, HBM],
        out_specs=(VMEM,) * 2,
        scratch_shapes=[
            pltpu.VMEM((2, members, columns, levels, features), BF16),
            pltpu.SemaphoreType.DMA((2,)),
        ],
        compiler_params=room(2),
        name="rows",
    )(band_rows, tokens)


def edges_kernel(band_ref, tokens_ref, west_ref, east_ref, cols, sem):
    slots, columns = tokens_ref.shape[1:3]
    odd, _ = band(band_ref)
    copies = [
        pltpu.make_async_copy(tokens_ref.at[:, :, column], cols.at[i], sem.at[i])
        for i, column in enumerate((0, columns - 1))
    ]
    for copy in copies:
        copy.start()
    for side, out_ref in enumerate((west_ref, east_ref)):
        copies[side].wait()
        out_ref[pl.ds(odd, slots)] = joined(cols[side])


def edges_of(band_rows, tokens):
    members, slots, _, levels, features = tokens.shape
    col = jax.ShapeDtypeStruct((slots + 2, levels, members * features), BF16)
    return pl.pallas_call(
        edges_kernel,
        out_shape=(col, col),
        in_specs=[SMEM, HBM],
        out_specs=(VMEM,) * 2,
        scratch_shapes=[
            pltpu.VMEM((2, members, slots, levels, features), BF16),
            pltpu.SemaphoreType.DMA((2,)),
        ],
        compiler_params=room(2),
        name="edges",
    )(band_rows, tokens)


def corners_kernel(band_ref, above_ref, below_ref, west_in, east_in, *out_refs):
    odd, live = band(band_ref)
    columns = above_ref.shape[0]
    west_ref, east_ref, near_ref, far_ref = out_refs
    west_ref[...] = west_in[...]
    east_ref[...] = east_in[...]
    for column, out_ref in ((0, west_ref), (columns - 1, east_ref)):
        out_ref[pl.ds(live + odd, 1)] = below_ref[pl.ds(column, 1)]

        @pl.when(odd == 1)
        def _():
            out_ref[pl.ds(0, 1)] = above_ref[pl.ds(column, 1)]

    even = lax.rem(lax.axis_index("lon"), 2) == 0

    @pl.when(even)
    def _():
        near_ref[...] = east_ref[...]
        far_ref[...] = west_ref[...]

    @pl.when(jnp.logical_not(even))
    def _():
        near_ref[...] = west_ref[...]
        far_ref[...] = east_ref[...]


def with_corners(band_rows, above, below, west, east):
    out = jax.ShapeDtypeStruct(west.shape, BF16)
    return pl.pallas_call(
        corners_kernel,
        out_shape=(out,) * 4,
        in_specs=[SMEM] + [VMEM] * 4,
        out_specs=(VMEM,) * 4,
        compiler_params=room(1),
        name="corners",
    )(band_rows, above, below, west, east)


def stacked(pieces, lengths):
    def kernel(*refs):
        start = 0
        for ref, length in zip(refs[:-1], lengths):
            refs[-1][start : start + length] = ref[:length]
            start += length

    return pl.pallas_call(
        kernel,
        out_shape=jax.ShapeDtypeStruct((sum(lengths),) + pieces[0].shape[1:], BF16),
        in_specs=[VMEM] * len(pieces),
        out_specs=VMEM,
        compiler_params=room(1),
        name="stacked",
    )(*pieces)


def merge_normed(parts, gain_ref, shift_ref):
    features = parts[0].shape[-1]
    total = parts[0] + parts[1] + parts[2] + parts[3]
    average = jnp.sum(total, axis=-1, keepdims=True) / (4 * features)
    parts = [part - average for part in parts]
    squares = parts[0] * parts[0]
    for part in parts[1:]:
        squares = squares + part * part
    spread = jnp.sum(squares, axis=-1, keepdims=True) / (4 * features)
    scale = lax.rsqrt(spread + EPS)
    return [
        (part * scale * gain_ref[k] + shift_ref[k]).astype(BF16) for k, part in enumerate(parts)
    ]


def group_sums(width, features):
    shape = (width, 2 * LANES)
    first = lax.broadcasted_iota(jnp.int32, shape, 0) < features
    low = lax.broadcasted_iota(jnp.int32, shape, 1) < LANES
    return jnp.where(first == low, 1.0, 0.0).astype(BF16)


def blended(low, high, rest):
    lane = lax.broadcasted_iota(jnp.int32, low.shape, 1)
    return jnp.concatenate([low, jnp.where(lane < rest, low, high), high], axis=-1)


def window(rows, q):
    return rows[:, q * LANES : q * LANES + 2 * LANES]


def mixed_pair(grown, sums, gain_ref, shift_ref, mix_ref, features):
    squares = (grown * grown).astype(BF16)
    spread = jnp.dot(squares, sums, preferred_element_type=F32)
    scale = lax.rsqrt(spread * (1.0 / features) + EPS)
    scale = blended(scale[:, :LANES], scale[:, LANES:], features - LANES)
    normed = (grown * scale * gain_ref[...] + shift_ref[...]).astype(BF16)
    return [padded_dot(window(normed, q), mix_ref, q) for q in range(2)]


def padded_dot(rows, weight_ref, q):
    start = (1 - q) * PAD
    weight = weight_ref[start : start + 2 * LANES]
    return jnp.dot(rows, weight, preferred_element_type=F32)


def cleared(band_ref, fine):
    odd, live = band(band_ref)
    members, rows = fine.shape[:2]

    def clear(row, carry):
        fine[:, pl.ds(row, 1)] = jnp.zeros((members, 1) + fine.shape[2:], BF16)
        return carry

    lax.fori_loop(live + odd, rows, clear, 0)
    return odd


def inner_norm_kernel(
    band_ref, tokens_ref, above_ref, below_ref, gain_ref, shift_ref, out_ref, field, sem
):
    members, slots, columns, levels, features = tokens_ref.shape
    half_rows, inner = slots // 2 + 1, columns - 2
    odd, live = band(band_ref)
    load = pltpu.make_async_copy(
        tokens_ref.at[:, :, pl.ds(1, inner)], field.at[:, pl.ds(odd, slots)], sem
    )
    load.start()
    load.wait()
    for member in range(members):
        lanes = slice(member * features, (member + 1) * features)

        @pl.when(odd == 1)
        def _():
            row = above_ref[1 : columns - 1].astype(F32)[..., lanes]
            field[member, pl.ds(0, 1)] = row.astype(BF16)[None]

        row = below_ref[1 : columns - 1].astype(F32)[..., lanes]
        field[member, pl.ds(live + odd, 1)] = row.astype(BF16)[None]
    pairs = field.reshape(members, half_rows, 2, inner // 2, 2, levels, features)
    step = out_ref.shape[1] // (members * inner // 2 * levels)

    def chunk(index, carry):
        parts = [
            pairs[:, pl.ds(index * step, step), p, :, q].astype(F32).reshape(-1, features)
            for q, p in ORDER
        ]
        out_ref[index] = jnp.concatenate(merge_normed(parts, gain_ref, shift_ref), axis=-1)
        return carry

    lax.fori_loop(0, out_ref.shape[0], chunk, 0)


def steps_of(half_rows):
    return max(step for step in range(1, 7) if half_rows % step == 0)


def inner_norm(band_rows, tokens, above, below, gain, shift):
    members, slots, columns, levels, features = tokens.shape
    half_rows, inner = slots // 2 + 1, columns - 2
    step = steps_of(half_rows)
    rows = step * members * inner // 2 * levels
    return pl.pallas_call(
        inner_norm_kernel,
        out_shape=jax.ShapeDtypeStruct((half_rows // step, rows, 4 * features), BF16),
        in_specs=[SMEM, HBM] + [VMEM] * 4,
        out_specs=VMEM,
        scratch_shapes=[
            pltpu.VMEM((members, slots + 2, inner, levels, features), BF16),
            pltpu.SemaphoreType.DMA,
        ],
        cost_estimate=cost(10**9, 10**6),
        compiler_params=room(10),
        name="inner_norm",
    )(band_rows, tokens, above, below, gain, shift)


def inner_kernel(
    band_ref, normed_ref, down_ref, up_ref, gain_ref, shift_ref, mix_ref, out_ref, fine, sem
):
    members, slots, columns, levels, features = out_ref.shape
    half_rows, inner = slots // 2 + 1, columns - 2
    count = normed_ref.shape[0]
    step = half_rows // count
    pairs = fine.reshape(members, half_rows, 2, inner // 2, 2, levels, features)
    sums = group_sums(2 * features, features)

    def chunk(index, carry):
        down = jnp.concatenate([down_ref[k, PAD : PAD + features] for k in range(4)], axis=0)
        coarse = jnp.dot(normed_ref[index], down, preferred_element_type=F32).astype(BF16)
        for p in range(2):
            grown = jnp.dot(coarse, up_ref[p], preferred_element_type=F32)
            pair = mixed_pair(grown, sums, gain_ref, shift_ref, mix_ref, features)
            for q, mixed in enumerate(pair):
                mixed = mixed.reshape(members, step, inner // 2, levels, features)
                pairs[:, pl.ds(index * step, step), p, :, q] = mixed.astype(BF16)
        return carry

    lax.fori_loop(0, count, chunk, 0)
    odd = cleared(band_ref, fine)
    store = pltpu.make_async_copy(
        fine.at[:, pl.ds(odd, slots)], out_ref.at[:, :, pl.ds(1, inner)], sem
    )
    store.start()
    store.wait()


def inner_of(band_rows, normed, down, up, gain, shift, mix, shape):
    members, slots, columns, levels, features = shape
    return pl.pallas_call(
        inner_kernel,
        out_shape=jax.ShapeDtypeStruct(shape, BF16),
        in_specs=[SMEM] + [VMEM] * 6,
        out_specs=HBM,
        scratch_shapes=[
            pltpu.VMEM((members, slots + 2, columns - 2, levels, features), BF16),
            pltpu.SemaphoreType.DMA,
        ],
        cost_estimate=cost(4 * 10**9, 10**6),
        compiler_params=room(16),
        name="inner",
    )(band_rows, normed, down, up, gain, shift, mix)


def rows_at(ref, p):
    rows, levels, width = ref.shape
    half = ref.reshape(rows // 2, 2, levels, width)[:, p]
    return half.astype(F32).reshape(-1, width)


def member_means(values, lower, count):
    middle = values[:, LANES : 2 * LANES]
    zero = jnp.zeros_like(middle)
    first = values[:, :LANES] + jnp.where(lower, middle, zero)
    second = values[:, 2 * LANES :] + jnp.where(lower, zero, middle)
    return [
        jnp.broadcast_to(jnp.sum(half, axis=-1, keepdims=True) / count, middle.shape)
        for half in (first, second)
    ]


def outer_kernel(
    band_ref,
    near_ref,
    west_ref,
    east_ref,
    far_ref,
    gain_ref,
    shift_ref,
    down_ref,
    up_ref,
    up_gain_ref,
    up_shift_ref,
    mix_ref,
    partial_ref,
    out_ref,
    fine,
    sem,
):
    del partial_ref
    members, slots, columns, levels, features = out_ref.shape
    half_rows = slots // 2 + 1
    odd, _ = band(band_ref)
    copies = []
    width = members * features
    lane = lax.broadcasted_iota(jnp.int32, (half_rows * levels, LANES), 1)
    lower = lane < features - LANES
    sums = group_sums(width, features)
    even = lax.rem(lax.axis_index("lon"), 2) == 0
    for side in range(2):
        parts = []
        for q, p in ORDER:
            ref = (west_ref, east_ref)[side] if q != side else None
            if ref is not None:
                part = rows_at(ref, p)
            else:
                part = jnp.where(even == (side == 0), rows_at(far_ref, p), rows_at(near_ref, p))
            parts.append(part)
        averages = member_means(parts[0] + parts[1] + parts[2] + parts[3], lower, 4 * features)
        average = blended(*averages, features - LANES)
        parts = [part - average for part in parts]
        squares = parts[0] * parts[0]
        for part in parts[1:]:
            squares = squares + part * part
        spreads = member_means(squares, lower, 4 * features)
        scale = blended(*(lax.rsqrt(spread + EPS) for spread in spreads), features - LANES)
        coarse = [None] * members
        for k, part in enumerate(parts):
            normed = (part * scale * gain_ref[k] + shift_ref[k]).astype(BF16)
            for member in range(members):
                term = padded_dot(window(normed, member), down_ref.at[k], member)
                coarse[member] = term if coarse[member] is None else coarse[member] + term
        coarse = jnp.concatenate(coarse, axis=0).astype(BF16)
        q = 1 - side
        lanes = slice(q * LANES, q * LANES + 2 * LANES)
        for p in range(2):
            grown = jnp.dot(coarse, up_ref[p, :, lanes], preferred_element_type=F32)
            squares = (grown * grown).astype(BF16)
            spread = jnp.dot(squares, sums[lanes, q * LANES : (q + 1) * LANES], preferred_element_type=F32)
            scale = lax.rsqrt(spread * (1.0 / features) + EPS)
            scale = jnp.concatenate([scale, scale], axis=-1)
            normed = grown * scale * up_gain_ref[:, lanes] + up_shift_ref[:, lanes]
            mixed = padded_dot(normed.astype(BF16), mix_ref, q)
            mixed = mixed.reshape(members, half_rows, levels, features)
            view = fine.at[side].reshape(members, half_rows, 2, levels, features)
            view[:, :, p] = mixed.astype(BF16)
        cleared(band_ref, fine.at[side])
        copy = pltpu.make_async_copy(
            fine.at[side, :, pl.ds(odd, slots)],
            out_ref.at[:, :, side * (columns - 1)],
            sem.at[side],
        )
        copy.start()
        copies.append(copy)
    for copy in copies:
        copy.wait()


def outer_of(band_rows, sides, gain, shift, down, up, up_gain, up_shift, mix, partial):
    members, slots, _, levels, features = partial.shape
    return pl.pallas_call(
        outer_kernel,
        out_shape=jax.ShapeDtypeStruct(partial.shape, BF16),
        in_specs=[SMEM] + [VMEM] * 11 + [HBM],
        out_specs=HBM,
        scratch_shapes=[
            pltpu.VMEM((2, members, slots + 2, levels, features), BF16),
            pltpu.SemaphoreType.DMA((2,)),
        ],
        input_output_aliases={12: 0},
        cost_estimate=cost(3 * 10**9, 10**6),
        compiler_params=room(12),
        name="outer",
    )(band_rows, *sides, gain, shift, down, up, up_gain, up_shift, mix, partial)


def assemble_kernel(*refs):
    pieces, (down_ref, up_ref) = refs[:-2], refs[-2:]
    pad = PAD // 8
    _, lat, up_tiles = up_ref.shape[1:4]
    own = pieces[0]
    tiles = own.shape[0] - 2 * up_tiles
    zero = jnp.zeros((pad,) + own.shape[1:], BF16)
    for part in range(down_ref.shape[0]):
        down_ref[part, :pad] = zero
        down_ref[part, pad + lat * tiles :] = zero
    here, place = lax.axis_index("lon"), lax.axis_index("lat")
    own, z1, z2, z3, core, across, across12, across3, rest, last = pieces
    far = lat - 1 - place
    beside = lax.bitwise_xor(place, 1)
    beside_far = lat - 1 - beside
    n = tiles + 2 * up_tiles
    table = [
        (own, 0, 0, place),
        (z1, 0, 1, place),
        (z2, 0, 2, place),
        (z3, 0, 3, place),
        (core, 0, 0, beside),
        (across, 0, 0, far),
        (across12, 0, 1, far),
        (across12, n, 2, far),
        (across3, 0, 3, far),
        (rest, 0, 1, beside),
        (rest, n, 2, beside),
        (rest, 2 * n, 3, beside),
        (rest, 3 * n, 0, beside_far),
        (rest, 4 * n, 1, beside_far),
        (rest, 5 * n, 2, beside_far),
        (last, 0, 3, beside_far),
    ]
    for ref, at, hop, row in table:
        source = lax.bitwise_xor(here, hop)
        down_ref[source, pl.ds(pad + row * tiles, tiles)] = ref[at : at + tiles]
        up_ref[0, source, row] = ref[at + tiles : at + tiles + up_tiles]
        up_ref[1, source, row] = ref[at + tiles + up_tiles : at + n]


def fast_weights(band_rows, tokens, down, up, features):
    lon, lat = lax.axis_size("lon"), lax.axis_size("lat")
    tiles, up_tiles = down.shape[0] // 8, up.shape[0] // 8
    place = lax.axis_index("lat")
    beside, mirror = lambda i: i ^ 1, lambda i: lat - 1 - i
    shard, core, across = first_sends(band_rows, tokens, down, up)
    core = swapped(core, "lat", beside)
    across = swapped(across, "lat", mirror)
    z2 = swapped(shard, "lon", lambda i: i ^ 2)
    z3 = swapped(shard, "lon", lambda i: i ^ 3)
    z1 = swapped(shard, "lon", beside)
    even = place % 2 == 0
    n = shard.shape[0]
    core_rows, across_rows = core[n:], across[n:]
    below = jnp.where(even, core_rows, across_rows)
    below = jnp.where(place == lat - 1, jnp.zeros_like(below), below)
    above = jnp.where(even, across_rows, core_rows)
    across12 = swapped(jnp.concatenate([z1, z2]), "lat", mirror)
    across3 = swapped(z3, "lat", mirror)
    rest = stacked([z1, z2, z3, across, across12], [n, n, n, n, 2 * n])
    rest = swapped(rest, "lat", beside)
    final = swapped(across3, "lat", beside)
    down, up = pl.pallas_call(
        assemble_kernel,
        out_shape=(
            jax.ShapeDtypeStruct((lon, lat * tiles + PAD // 4, 8, down.shape[1]), BF16),
            jax.ShapeDtypeStruct((2, lon, lat, up_tiles, 8, down.shape[1]), BF16),
        ),
        in_specs=[VMEM] * 10,
        out_specs=(VMEM,) * 2,
        compiler_params=room(6),
        name="assemble",
    )(shard, z1, z2, z3, core, across, across12, across3, rest, final)
    down = down.reshape(4, -1, down.shape[-1])
    return down, up, above, below


def plain_weights(band_rows, tokens, down, up, features):
    first, last = rows_of(band_rows, tokens)
    up = centred(up, features)
    below = passed_along(first, "lat", -1)
    above = passed_along(last, "lat", 1)
    rows, half = up.shape[0], up.shape[1] // 2
    shard = jnp.concatenate([down, up[:, :half], up[:, half:]], axis=0)
    whole = lax.all_gather(shard, ("lon", "lat"), axis=0)
    n = down.shape[0]
    up = jnp.stack([whole[:, n : n + rows], whole[:, n + rows :]])
    down = whole[:, :n].reshape(4, features, half)
    return jnp.pad(down, ((0, 0), (PAD, PAD), (0, 0))), up, above, below


def whole(
    tokens, band_rows, down_gain, down_shift, down_weight, up_weight, up_gain, up_shift, mix_weight
):
    _, _, _, _, features = tokens.shape
    lon, lat = lax.axis_size("lon"), lax.axis_size("lat")
    block = tokens.transpose(0, 2, 3, 1, 4)
    west, east = edges_of(band_rows, block)
    plain = lon != 4 or lat != 4 or down_weight.shape[0] % 8 or up_weight.shape[0] % 8
    weights = plain_weights if plain else fast_weights
    down, up, above, below = weights(band_rows, block, down_weight, up_weight, features)
    narrow = down_weight.shape[1]
    up = up.reshape(2, narrow, narrow)
    west, east, near, far = with_corners(band_rows, above, below, west, east)
    far = swapped(far, "lon", lambda i: (i - 1 if i % 2 == 0 else i + 1) % lon)
    near = swapped(near, "lon", lambda i: i ^ 1)
    gain, shift = down_gain.reshape(4, 1, features), down_shift.reshape(4, 1, features)
    twice = lambda value: jnp.concatenate([value, value], axis=-1)
    fine_gain, fine_shift = twice(up_gain)[None], twice(up_shift)[None]
    mix_weight = jnp.pad(mix_weight, ((PAD, PAD), (0, 0)))
    normed = inner_norm(band_rows, block, above, below, gain, shift)
    out = inner_of(
        band_rows, normed, down, up, fine_gain, fine_shift, mix_weight, block.shape
    )
    out = outer_of(
        band_rows,
        (near, west, east, far),
        twice(gain),
        twice(shift),
        down,
        up,
        fine_gain,
        fine_shift,
        mix_weight,
        out,
    )
    return out.transpose(0, 3, 1, 2, 4)


def solution(mesh):
    return jax.shard_map(
        whole,
        mesh=mesh,
        in_specs=(
            P("mem", None, "lat", "lon", None),
            P("lat", None),
            P(),
            P(),
            P(("lon", "lat"), None),
            P(("lon", "lat"), None),
            P(),
            P(),
            P(),
        ),
        out_specs=P("mem", None, "lat", "lon", None),
        check_vma=False,
    )
```

profile of v0, /device:TPU:0, one launch (start us, length us, event | category | flops | bytes accessed | tf_op | source)
XLA Modules:
  0.0 52.1 jit_solution(17685442520827239864)
XLA Ops:
  0.0 1.5 %copy-done = bf16[2,8,34,6,192]{4,1,3,2,0:T(8,128)(2,1)S(1)} copy-done((bf16[2,8,34,6,192]{4,1,3,2,0:T(8,128)(2,1)S(1)}, bf16[2,8,34,6,192]{4,1,3,2,0:T(8,128)(2,1)}, u32[]{:S(2)}) %copy-start) | copy-done | bytes 1253400
  1.5 0.8 %copy-done.2 = bf16[48,384]{1,0:T(8,128)(2,1)S(1)} copy-done((bf16[48,384]{1,0:T(8,128)(2,1)S(1)}, bf16[48,384]{1,0:T(8,128)(2,1)}, u32[]{:S(2)}) %copy-start.2) | copy-done | bytes 36888
  2.3 0.8 %copy-done.3 = bf16[24,768]{1,0:T(8,128)(2,1)S(1)} copy-done((bf16[24,768]{1,0:T(8,128)(2,1)S(1)}, bf16[24,768]{1,0:T(8,128)(2,1)}, u32[]{:S(2)}) %copy-start.3) | copy-done | bytes 36888
  3.0 0.7 %copy-done.5 = s32[1,2]{1,0:T(1,128)S(1)} copy-done((s32[1,2]{1,0:T(1,128)S(1)}, s32[1,2]{1,0:T(1,128)}, u32[]{:S(2)}) %copy-start.5) | copy-done | bytes 32
  3.7 1.7 %first.1 = (bf16[12,8,384]{2,1,0:T(8,128)(2,1)S(1)}, bf16[18,8,384]{2,1,0:T(8,128)(2,1)}, bf16[18,8,384]{2,1,0:T(8,128)(2,1)S(1)}) custom-call(s32[1,2]{1,0:T(1,128)S(1)} %copy-done.5, bf16[2,34,6,8,192]{4,3,2,1,0:T(8,128)(2,1)S(1)} %bitcast.6, bf16[6,8,384]{2,1,0:T(8,128)(2,1)S(1)} %bitcast.9, bf16[3,8,768]{2,1,0:T(8,128)(2,1)S(1)} %bitcast.10), custom_call_target="tpu_custom_call" | custom-call | tf_op jit(solution)/shard_map/first/pallas_call | solution.py:91
  5.4 4.1 %collective-permute-start.5 = (bf16[12,8,384]{2,1,0:T(8,128)(2,1)S(1)}, bf16[12,8,384]{2,1,0:T(8,128)(2,1)S(1)}, u32[]{:S(2)}, u32[]{:S(2)}) collective-permute-start(bf16[12,8,384]{2,1,0:T(8,128)(2,1)S(1)} %get-tuple-element.24.refs_0_), channel_id=1, source_target_pairs={{0,16},{8,24},{16,0},{24,8},{1,17},{9,25},{17,1},{25,9},{2,18},{10... | collective-permute-start | bytes 221192 | tf_op jit(solution)/shard_map/ppermute | solution.py:28
  9.5 1.6 %collective-permute-start.4 = (bf16[12,8,384]{2,1,0:T(8,128)(2,1)S(1)}, bf16[12,8,384]{2,1,0:T(8,128)(2,1)S(1)}, u32[]{:S(2)}, u32[]{:S(2)}) collective-permute-start(bf16[12,8,384]{2,1,0:T(8,128)(2,1)S(1)} %get-tuple-element.24.refs_0_), channel_id=1, source_target_pairs={{0,8},{8,0},{16,24},{24,16},{1,9},{9,1},{17,25},{25,17},{2,10},{10... | collective-permute-start | bytes 221192 | tf_op jit(solution)/shard_map/ppermute | solution.py:28
  11.1 1.8 %collective-permute-done.5.refs_1_.refs_2_ = bf16[12,8,384]{2,1,0:T(8,128)(2,1)S(1)} collective-permute-done((bf16[12,8,384]{2,1,0:T(8,128)(2,1)S(1)}, bf16[12,8,384]{2,1,0:T(8,128)(2,1)S(1)}, u32[]{:S(2)}, u32[]{:S(2)}) %collective-permute-start.5) | collective-permute-done | bytes 73760 | tf_op jit(solution)/shard_map/ppermute | solution.py:28
  12.9 1.0 %collective-permute-done.4.refs_0_.refs_1_ = bf16[12,8,384]{2,1,0:T(8,128)(2,1)S(1)} collective-permute-done((bf16[12,8,384]{2,1,0:T(8,128)(2,1)S(1)}, bf16[12,8,384]{2,1,0:T(8,128)(2,1)S(1)}, u32[]{:S(2)}, u32[]{:S(2)}) %collective-permute-start.4) | collective-permute-done | bytes 73760 | tf_op jit(solution)/shard_map/ppermute | solution.py:28
  13.9 0.6 %collective-permute-start.7 = (bf16[24,8,384]{2,1,0:T(8,128)(2,1)S(1)}, bf16[24,8,384]{2,1,0:T(8,128)(2,1)S(1)}, u32[]{:S(2)}, u32[]{:S(2)}) collective-permute-start(bf16[24,8,384]{2,1,0:T(8,128)(2,1)S(1)} %pad_maximum_fusion), channel_id=1, source_target_pairs={{0,6},{2,4},{4,2},{6,0},{1,7},{3,5},{5,3},{7,1},{8,14},{10,12},{12... | collective-permute-start | bytes 442376 | tf_op jit(solution)/shard_map/ppermute | solution.py:28
  14.5 3.3 %collective-permute-start.6 = (bf16[12,8,384]{2,1,0:T(8,128)(2,1)S(1)}, bf16[12,8,384]{2,1,0:T(8,128)(2,1)S(1)}, u32[]{:S(2)}, u32[]{:S(2)}) collective-permute-start(bf16[12,8,384]{2,1,0:T(8,128)(2,1)S(1)} %get-tuple-element.24.refs_0_), channel_id=1, source_target_pairs={{0,24},{8,16},{16,8},{24,0},{1,25},{9,17},{17,9},{25,1},{2,26},{10... | collective-permute-start | bytes 221192 | tf_op jit(solution)/shard_map/ppermute | solution.py:28
  17.9 0.6 %collective-permute-start = (bf16[18,8,384]{2,1,0:T(8,128)(2,1)S(1)}, bf16[18,8,384]{2,1,0:T(8,128)(2,1)S(1)}, u32[]{:S(2)}, u32[]{:S(2)}) collective-permute-start(bf16[18,8,384]{2,1,0:T(8,128)(2,1)S(1)} %get-tuple-element.16), channel_id=1, source_target_pairs={{0,6},{2,4},{4,2},{6,0},{1,7},{3,5},{5,3},{7,1},{8,14},{10,12},{12... | collective-permute-start | bytes 331784 | tf_op jit(solution)/shard_map/ppermute | solution.py:28
  18.5 0.2 collective-permute-start.1
  18.7 0.0 copy-done.11
  18.7 0.7 %pad_maximum_fusion.3 = f32[384]{0:T(512)} fusion(f32[192]{0:T(256)S(1)} %copy-done.11), kind=kLoop, calls=%fused_computation.5 | loop fusion | flops 384 | bytes 2304 | tf_op jit(solution)/shard_map/concatenate | solution.py:607
  19.4 2.0 %collective-permute-done.6.refs_2_.refs_3_ = bf16[12,8,384]{2,1,0:T(8,128)(2,1)S(1)} collective-permute-done((bf16[12,8,384]{2,1,0:T(8,128)(2,1)S(1)}, bf16[12,8,384]{2,1,0:T(8,128)(2,1)S(1)}, u32[]{:S(2)}, u32[]{:S(2)}) %collective-permute-start.6) | collective-permute-done | bytes 73760 | tf_op jit(solution)/shard_map/ppermute | solution.py:28
  21.3 1.3 %collective-permute-done.refs_3_.refs_5_ = bf16[18,8,384]{2,1,0:T(8,128)(2,1)S(1)} collective-permute-done((bf16[18,8,384]{2,1,0:T(8,128)(2,1)S(1)}, bf16[18,8,384]{2,1,0:T(8,128)(2,1)S(1)}, u32[]{:S(2)}, u32[]{:S(2)}) %collective-permute-start) | collective-permute-done | bytes 110624 | tf_op jit(solution)/shard_map/ppermute | solution.py:28
  22.6 0.0 collective-permute-done.7.refs_4_.refs_6_
  22.6 0.5 %collective-permute-start.9 = (bf16[72,8,384]{2,1,0:T(8,128)(2,1)S(1)}, bf16[72,8,384]{2,1,0:T(8,128)(2,1)S(1)}, u32[]{:S(2)}, u32[]{:S(2)}) collective-permute-start(bf16[72,8,384]{2,1,0:T(8,128)(2,1)S(1)} %stacked.1), channel_id=1, source_target_pairs={{0,2},{2,0},{4,6},{6,4},{1,3},{3,1},{5,7},{7,5},{8,10},{10,8},{12,... | collective-permute-start | bytes 1327112 | tf_op jit(solution)/shard_map/ppermute | solution.py:28
  23.2 0.0 copy-done.12
  23.2 0.7 %pad_maximum_fusion.4 = f32[384]{0:T(512)} fusion(f32[192]{0:T(256)S(1)} %copy-done.12), kind=kLoop, calls=%fused_computation.6 | loop fusion | flops 384 | bytes 2304 | tf_op jit(solution)/shard_map/concatenate | solution.py:607
  23.8 0.0 copy-done.1
  23.8 0.8 %edges.1 = (bf16[36,8,384]{2,1,0:T(8,128)(2,1)S(1)}, bf16[36,8,384]{2,1,0:T(8,128)(2,1)S(1)}) custom-call(s32[1,2]{1,0:T(1,128)S(1)} %copy-done.6, bf16[2,34,6,8,192]{4,3,2,1,0:T(8,128)(2,1)S(1)} %bitcast.7), custom_call_target="tpu_custom_call" | custom-call | tf_op jit(solution)/shard_map/edges/pallas_call | solution.py:154
  24.7 1.3 %broadcast_in_dim.10.gain_ref.up_gain_ref = f32[1,384]{1,0:T(1,128)} reshape(f32[384]{0:T(512)} %pad_maximum_fusion.3) | data formatting | bytes 3072 | tf_op jit(solution)/shard_map/broadcast_in_dim | solution.py:608
  25.9 1.3 %broadcast_in_dim.11.shift_ref.up_shift_ref = f32[1,384]{1,0:T(1,128)} reshape(f32[384]{0:T(512)} %pad_maximum_fusion.4) | data formatting | bytes 3072 | tf_op jit(solution)/shard_map/broadcast_in_dim | solution.py:608
  27.2 0.8 %reshape.20.gain_ref = f32[4,1,192]{2,1,0:T(1,128)S(1)} reshape(f32[768]{0:T(1024)} %param.11) | data formatting | bytes 6144 | tf_op jit(solution)/shard_map/reshape | solution.py:606
  28.0 1.4 %reshape.21.shift_ref = f32[4,1,192]{2,1,0:T(1,128)} reshape(f32[768]{0:T(1024)} %param.12) | data formatting | bytes 6144 | tf_op jit(solution)/shard_map/reshape | solution.py:606
  29.3 0.9 %pad.4.mix_ref = bf16[320,192]{1,0:T(8,128)(2,1)S(1)} pad(bf16[192,192]{1,0:T(8,128)(2,1)} %param.17, bf16[]{:T(256)} %constant.24.clone.1), padding=64_64x0_0 | pad | bytes 196610 | tf_op jit(solution)/shard_map/jit(_pad)/pad | solution.py:609
  30.2 0.8 %pad_maximum_fusion.1 = (f32[4,1,384]{2,1,0:T(1,128)S(1)}, f32[4,1,384]{2,1,0:T(1,128)S(1)}) fusion(f32[4,1,192]{2,1,0:T(1,128)S(1)} %reshape.20.gain_ref, f32[4,1,192]{2,1,0:T(1,128)} %reshape.21.shift_ref), kind=kLoop, calls=%fused_computation.3 | loop fusion | flops 3072 | bytes 18432 | tf_op jit(solution)/shard_map/concatenate | solution.py:607
  31.1 0.6 %collective-permute-start.8 = (bf16[12,8,384]{2,1,0:T(8,128)(2,1)S(1)}, bf16[12,8,384]{2,1,0:T(8,128)(2,1)S(1)}, u32[]{:S(2)}, u32[]{:S(2)}) collective-permute-start(bf16[12,8,384]{2,1,0:T(8,128)(2,1)S(1)} %collective-permute-done.6.refs_2_.refs_3_), channel_id=1, source_target_pairs={{0,6},{2,4},{4,2},{6,0},{1,7},{3,5},{5,3},{7,1},{8,14},{10,12},{12... | collective-permute-start | bytes 221192 | tf_op jit(solution)/shard_map/ppermute | solution.py:28
  31.7 0.0 collective-permute-done.1.refs_4_
  31.7 0.8 %select_select_fusion = (bf16[6,8,384]{2,1,0:T(8,128)(2,1)S(1)}, bf16[6,8,384]{2,1,0:T(8,128)(2,1)S(1)}) fusion(pred[]{:T(512)S(6)} %eq.9, pred[]{:T(512)S(6)} %eq.8, bf16[18,8,384]{2,1,0:T(8,128)(2,1)} %collective-permute-done.1.refs_4_, bf16[18,8,384]{2,1,0:T(8,128)(2,1)S(1)} %collective-permute-done.refs_3_.refs_5_), kind=kLoop, calls=%fused_computation.1 | loop fusion | flops 55296 | bytes 147458 | tf_op jit(solution)/shard_map/jit(_where)/select_n | solution.py:555
  32.4 0.0 copy-start.7
  32.5 0.6 %copy-done.7 = s32[1,2]{1,0:T(1,128)S(1)} copy-done((s32[1,2]{1,0:T(1,128)S(1)}, s32[1,2]{1,0:T(1,128)}, u32[]{:S(2)}) %copy-start.7) | copy-done | bytes 32
  33.1 0.6 %corners.1 = (bf16[36,8,384]{2,1,0:T(8,128)(2,1)S(1)}, bf16[36,8,384]{2,1,0:T(8,128)(2,1)S(1)}, bf16[36,8,384]{2,1,0:T(8,128)(2,1)S(1)}, bf16[36,8,384]{2,1,0:T(8,128)(2,1)S(1)}) custom-call(s32[1,2]{1,0:T(1,128)S(1)} %copy-done.7, bf16[6,8,384]{2,1,0:T(8,128)(2,1)S(1)} %get-tuple-element.28.above_ref, bf16[6,8,384]{2,1,0:T(8,128)(2,1)S(1)} %get-tuple-element.27.below_ref, ...), custom_call_target="tpu_custom_call" | custom-call | tf_op jit(solution)/shard_map/corners/pallas_call | solution.py:196
  33.8 1.4 %collective-permute-start.2 = (bf16[36,8,384]{2,1,0:T(8,128)(2,1)S(1)}, bf16[36,8,384]{2,1,0:T(8,128)(2,1)S(1)}, u32[]{:S(2)}, u32[]{:S(2)}) collective-permute-start(bf16[36,8,384]{2,1,0:T(8,128)(2,1)S(1)} %get-tuple-element.20), channel_id=1, source_target_pairs={{0,8},{8,0},{16,24},{24,16},{1,9},{9,1},{17,25},{25,17},{2,10},{10... | collective-permute-start | bytes 663560 | tf_op jit(solution)/shard_map/ppermute | solution.py:28
  35.1 2.3 %collective-permute-start.3 = (bf16[36,8,384]{2,1,0:T(8,128)(2,1)S(1)}, bf16[36,8,384]{2,1,0:T(8,128)(2,1)S(1)}, u32[]{:S(2)}, u32[]{:S(2)}) collective-permute-start(bf16[36,8,384]{2,1,0:T(8,128)(2,1)S(1)} %get-tuple-element.23), channel_id=1, source_target_pairs={{0,24},{8,16},{16,8},{24,0},{1,25},{9,17},{17,9},{25,1},{2,26},{10... | collective-permute-start | bytes 663560 | tf_op jit(solution)/shard_map/ppermute | solution.py:28
  37.4 0.0 collective-permute-done.8.refs_7_
  37.4 0.0 collective-permute-start.10
  37.4 0.7 %copy-done.4 = f32[4,1,192]{2,1,0:T(1,128)S(1)} copy-done((f32[4,1,192]{2,1,0:T(1,128)S(1)}, f32[4,1,192]{2,1,0:T(1,128)}, u32[]{:S(2)}) %copy-start.4) | copy-done | bytes 3096
  38.1 1.9 %inner_norm.1.normed_ref = bf16[3,192,768]{2,1,0:T(8,128)(2,1)S(1)} custom-call(s32[1,2]{1,0:T(1,128)S(1)} %copy-done.7, bf16[2,34,6,8,192]{4,3,2,1,0:T(8,128)(2,1)S(1)} %bitcast.8, bf16[6,8,384]{2,1,0:T(8,128)(2,1)S(1)} %get-tuple-element.28.above_ref, bf16[6,8,384]{2,1,0:T(8,128)(2,1)S(1)} %get-tuple-element.27.below_ref, ...), custom_call_target="tpu_custom_call" | custom-call | flops 1000000000 | bytes 1000000 | tf_op jit(solution)/shard_map/inner_norm/pallas_call | solution.py:325
  40.0 0.0 collective-permute-done.10.refs_9_
  40.0 0.0 collective-permute-done.9.refs_8_
  40.0 1.0 %assemble.1 = (bf16[4,40,8,384]{3,2,1,0:T(8,128)(2,1)S(1)}, bf16[2,4,4,3,8,384]{5,4,3,2,1,0:T(8,128)(2,1)S(1)}) custom-call(bf16[12,8,384]{2,1,0:T(8,128)(2,1)S(1)} %get-tuple-element.24.refs_0_, bf16[12,8,384]{2,1,0:T(8,128)(2,1)S(1)} %collective-permute-done.4.refs_0_.refs_1_, bf16[12,8,384]{2,1,0:T(8,128)(2,1)S(1)} %collective-permute-done.5.refs_1_.refs_2_, ...), custom_call_target="tpu_custom_call" | custom-call | tf_op jit(solution)/shard_map/assemble/pallas_call | solution.py:562
  41.1 5.4 %inner.1.partial_ref = bf16[2,34,6,8,192]{4,3,2,1,0:T(8,128)(2,1)} custom-call(s32[1,2]{1,0:T(1,128)S(1)} %copy-done.8, bf16[3,192,768]{2,1,0:T(8,128)(2,1)S(1)} %inner_norm.1.normed_ref, bf16[4,320,384]{2,1,0:T(8,128)(2,1)S(1)} %bitcast.11, bf16[2,384,384]{2,1,0:T(8,128)(2,1)S(1)} %bitcast.13, f32[1,384]{1,0:T(1,128)S(1)} %copy-done.9, ...), custom_call_target="tpu_custom_call" | custom-call | flops 4000000000 | bytes 1000000 | tf_op jit(solution)/shard_map/inner/pallas_call | solution.py:372
  46.6 0.0 collective-permute-done.2.near_ref
  46.6 1.3 %collective-permute-done.3.far_ref = bf16[36,8,384]{2,1,0:T(8,128)(2,1)S(1)} collective-permute-done((bf16[36,8,384]{2,1,0:T(8,128)(2,1)S(1)}, bf16[36,8,384]{2,1,0:T(8,128)(2,1)S(1)}, u32[]{:S(2)}, u32[]{:S(2)}) %collective-permute-start.3) | collective-permute-done | bytes 221216 | tf_op jit(solution)/shard_map/ppermute | solution.py:28
  47.8 4.3 %outer.1 = bf16[2,34,6,8,192]{4,3,2,1,0:T(8,128)(2,1)} custom-call(s32[1,2]{1,0:T(1,128)S(1)} %copy-done.8, bf16[36,8,384]{2,1,0:T(8,128)(2,1)S(1)} %collective-permute-done.2.near_ref, bf16[36,8,384]{2,1,0:T(8,128)(2,1)S(1)} %get-tuple-element.21.west_ref, bf16[36,8,384]{2,1,0:T(8,128)(2,1)S(1)} %get-tuple-element.22.east_ref, ...), custom_call_target="tpu_custom_call", output_to_operand_aliasing={{}: (12, {})} | custom-call | flops 3000000000 | bytes 1000000 | tf_op jit(solution)/shard_map/outer/pallas_call | solution.py:483
  (18 shorter events, 0.1 us)
Async XLA Ops:
  0.0 23.8 %copy-start.6 = (s32[1,2]{1,0:T(1,128)S(1)}, s32[1,2]{1,0:T(1,128)}, u32[]{:S(2)}) copy-start(s32[1,2]{1,0:T(1,128)} %band_ref.11) | copy-start | bytes 28
  0.0 18.7 %copy-start.11 = (f32[192]{0:T(256)S(1)}, f32[192]{0:T(256)}, u32[]{:S(2)}) copy-start(f32[192]{0:T(256)} %param.15) | copy-start | bytes 2308
  0.0 23.2 %copy-start.12 = (f32[192]{0:T(256)S(1)}, f32[192]{0:T(256)}, u32[]{:S(2)}) copy-start(f32[192]{0:T(256)} %param.16) | copy-start | bytes 2308
  0.0 1.5 %copy-start = (bf16[2,8,34,6,192]{4,1,3,2,0:T(8,128)(2,1)S(1)}, bf16[2,8,34,6,192]{4,1,3,2,0:T(8,128)(2,1)}, u32[]{:S(2)}) copy-start(bf16[2,8,34,6,192]{4,1,3,2,0:T(8,128)(2,1)} %param.9) | copy-start | bytes 3760132
  1.5 0.8 %copy-start.2 = (bf16[48,384]{1,0:T(8,128)(2,1)S(1)}, bf16[48,384]{1,0:T(8,128)(2,1)}, u32[]{:S(2)}) copy-start(bf16[48,384]{1,0:T(8,128)(2,1)} %param.13) | copy-start | bytes 110596
  2.3 0.8 %copy-start.3 = (bf16[24,768]{1,0:T(8,128)(2,1)S(1)}, bf16[24,768]{1,0:T(8,128)(2,1)}, u32[]{:S(2)}) copy-start(bf16[24,768]{1,0:T(8,128)(2,1)} %param.14) | copy-start | bytes 110596
  3.0 0.7 %copy-start.5 = (s32[1,2]{1,0:T(1,128)S(1)}, s32[1,2]{1,0:T(1,128)}, u32[]{:S(2)}) copy-start(s32[1,2]{1,0:T(1,128)} %band_ref.11) | copy-start | bytes 28
  3.7 20.2 %copy-start.1 = (bf16[2,8,34,6,192]{4,1,3,2,0:T(8,128)(2,1)S(1)}, bf16[2,8,34,6,192]{4,1,3,2,0:T(8,128)(2,1)}, u32[]{:S(2)}) copy-start(bf16[2,8,34,6,192]{4,1,3,2,0:T(8,128)(2,1)} %param.9) | copy-start | bytes 3760132
  5.4 7.5 %collective-permute-start.5 = (bf16[12,8,384]{2,1,0:T(8,128)(2,1)S(1)}, bf16[12,8,384]{2,1,0:T(8,128)(2,1)S(1)}, u32[]{:S(2)}, u32[]{:S(2)}) collective-permute-start(bf16[12,8,384]{2,1,0:T(8,128)(2,1)S(1)} %get-tuple-element.24.refs_0_), channel_id=1, source_target_pairs={{0,16},{8,24},{16,0},{24,8},{1,17},{9,25},{17,1},{25,9},{2,18},{10... | collective-permute-start | bytes 221192 | tf_op jit(solution)/shard_map/ppermute | solution.py:28
  9.5 4.4 %collective-permute-start.4 = (bf16[12,8,384]{2,1,0:T(8,128)(2,1)S(1)}, bf16[12,8,384]{2,1,0:T(8,128)(2,1)S(1)}, u32[]{:S(2)}, u32[]{:S(2)}) collective-permute-start(bf16[12,8,384]{2,1,0:T(8,128)(2,1)S(1)} %get-tuple-element.24.refs_0_), channel_id=1, source_target_pairs={{0,8},{8,0},{16,24},{24,16},{1,9},{9,1},{17,25},{25,17},{2,10},{10... | collective-permute-start | bytes 221192 | tf_op jit(solution)/shard_map/ppermute | solution.py:28
  13.9 8.7 %collective-permute-start.7 = (bf16[24,8,384]{2,1,0:T(8,128)(2,1)S(1)}, bf16[24,8,384]{2,1,0:T(8,128)(2,1)S(1)}, u32[]{:S(2)}, u32[]{:S(2)}) collective-permute-start(bf16[24,8,384]{2,1,0:T(8,128)(2,1)S(1)} %pad_maximum_fusion), channel_id=1, source_target_pairs={{0,6},{2,4},{4,2},{6,0},{1,7},{3,5},{5,3},{7,1},{8,14},{10,12},{12... | collective-permute-start | bytes 442376 | tf_op jit(solution)/shard_map/ppermute | solution.py:28
  14.5 6.8 %collective-permute-start.6 = (bf16[12,8,384]{2,1,0:T(8,128)(2,1)S(1)}, bf16[12,8,384]{2,1,0:T(8,128)(2,1)S(1)}, u32[]{:S(2)}, u32[]{:S(2)}) collective-permute-start(bf16[12,8,384]{2,1,0:T(8,128)(2,1)S(1)} %get-tuple-element.24.refs_0_), channel_id=1, source_target_pairs={{0,24},{8,16},{16,8},{24,0},{1,25},{9,17},{17,9},{25,1},{2,26},{10... | collective-permute-start | bytes 221192 | tf_op jit(solution)/shard_map/ppermute | solution.py:28
  17.9 4.7 %collective-permute-start = (bf16[18,8,384]{2,1,0:T(8,128)(2,1)S(1)}, bf16[18,8,384]{2,1,0:T(8,128)(2,1)S(1)}, u32[]{:S(2)}, u32[]{:S(2)}) collective-permute-start(bf16[18,8,384]{2,1,0:T(8,128)(2,1)S(1)} %get-tuple-element.16), channel_id=1, source_target_pairs={{0,6},{2,4},{4,2},{6,0},{1,7},{3,5},{5,3},{7,1},{8,14},{10,12},{12... | collective-permute-start | bytes 331784 | tf_op jit(solution)/shard_map/ppermute | solution.py:28
  18.5 13.2 %collective-permute-start.1 = (bf16[18,8,384]{2,1,0:T(8,128)(2,1)}, bf16[18,8,384]{2,1,0:T(8,128)(2,1)}, u32[]{:S(2)}, u32[]{:S(2)}) collective-permute-start(bf16[18,8,384]{2,1,0:T(8,128)(2,1)} %get-tuple-element.17), channel_id=1, source_target_pairs={{0,2},{2,0},{4,6},{6,4},{1,3},{3,1},{5,7},{7,5},{8,10},{10,8},{12,... | collective-permute-start | bytes 331784 | tf_op jit(solution)/shard_map/ppermute | solution.py:28
  22.6 17.4 %collective-permute-start.9 = (bf16[72,8,384]{2,1,0:T(8,128)(2,1)S(1)}, bf16[72,8,384]{2,1,0:T(8,128)(2,1)S(1)}, u32[]{:S(2)}, u32[]{:S(2)}) collective-permute-start(bf16[72,8,384]{2,1,0:T(8,128)(2,1)S(1)} %stacked.1), channel_id=1, source_target_pairs={{0,2},{2,0},{4,6},{6,4},{1,3},{3,1},{5,7},{7,5},{8,10},{10,8},{12,... | collective-permute-start | bytes 1327112 | tf_op jit(solution)/shard_map/ppermute | solution.py:28
  31.1 6.3 %collective-permute-start.8 = (bf16[12,8,384]{2,1,0:T(8,128)(2,1)S(1)}, bf16[12,8,384]{2,1,0:T(8,128)(2,1)S(1)}, u32[]{:S(2)}, u32[]{:S(2)}) collective-permute-start(bf16[12,8,384]{2,1,0:T(8,128)(2,1)S(1)} %collective-permute-done.6.refs_2_.refs_3_), channel_id=1, source_target_pairs={{0,6},{2,4},{4,2},{6,0},{1,7},{3,5},{5,3},{7,1},{8,14},{10,12},{12... | collective-permute-start | bytes 221192 | tf_op jit(solution)/shard_map/ppermute | solution.py:28
  32.4 0.7 %copy-start.7 = (s32[1,2]{1,0:T(1,128)S(1)}, s32[1,2]{1,0:T(1,128)}, u32[]{:S(2)}) copy-start(s32[1,2]{1,0:T(1,128)} %band_ref.11) | copy-start | bytes 28
  33.8 12.8 %collective-permute-start.2 = (bf16[36,8,384]{2,1,0:T(8,128)(2,1)S(1)}, bf16[36,8,384]{2,1,0:T(8,128)(2,1)S(1)}, u32[]{:S(2)}, u32[]{:S(2)}) collective-permute-start(bf16[36,8,384]{2,1,0:T(8,128)(2,1)S(1)} %get-tuple-element.20), channel_id=1, source_target_pairs={{0,8},{8,0},{16,24},{24,16},{1,9},{9,1},{17,25},{25,17},{2,10},{10... | collective-permute-start | bytes 663560 | tf_op jit(solution)/shard_map/ppermute | solution.py:28
  35.1 6.0 %copy-start.8 = (s32[1,2]{1,0:T(1,128)S(1)}, s32[1,2]{1,0:T(1,128)}, u32[]{:S(2)}) copy-start(s32[1,2]{1,0:T(1,128)} %band_ref.11) | copy-start | bytes 28
  35.1 12.7 %collective-permute-start.3 = (bf16[36,8,384]{2,1,0:T(8,128)(2,1)S(1)}, bf16[36,8,384]{2,1,0:T(8,128)(2,1)S(1)}, u32[]{:S(2)}, u32[]{:S(2)}) collective-permute-start(bf16[36,8,384]{2,1,0:T(8,128)(2,1)S(1)} %get-tuple-element.23), channel_id=1, source_target_pairs={{0,24},{8,16},{16,8},{24,0},{1,25},{9,17},{17,9},{25,1},{2,26},{10... | collective-permute-start | bytes 663560 | tf_op jit(solution)/shard_map/ppermute | solution.py:28
  37.4 2.6 %collective-permute-start.10 = (bf16[12,8,384]{2,1,0:T(8,128)(2,1)S(1)}, bf16[12,8,384]{2,1,0:T(8,128)(2,1)S(1)}, u32[]{:S(2)}, u32[]{:S(2)}) collective-permute-start(bf16[12,8,384]{2,1,0:T(8,128)(2,1)S(1)} %collective-permute-done.8.refs_7_), channel_id=1, source_target_pairs={{0,2},{2,0},{4,6},{6,4},{1,3},{3,1},{5,7},{7,5},{8,10},{10,8},{12,... | collective-permute-start | bytes 221192 | tf_op jit(solution)/shard_map/ppermute | solution.py:28
  37.4 0.7 %copy-start.4 = (f32[4,1,192]{2,1,0:T(1,128)S(1)}, f32[4,1,192]{2,1,0:T(1,128)}, u32[]{:S(2)}) copy-start(f32[4,1,192]{2,1,0:T(1,128)} %reshape.21.shift_ref) | copy-start | bytes 9220
  38.1 3.0 %copy-start.9 = (f32[1,384]{1,0:T(1,128)S(1)}, f32[1,384]{1,0:T(1,128)}, u32[]{:S(2)}) copy-start(f32[1,384]{1,0:T(1,128)} %broadcast_in_dim.10.gain_ref.up_gain_ref) | copy-start | bytes 4612
  38.1 3.0 %copy-start.10 = (f32[1,384]{1,0:T(1,128)S(1)}, f32[1,384]{1,0:T(1,128)}, u32[]{:S(2)}) copy-start(f32[1,384]{1,0:T(1,128)} %broadcast_in_dim.11.shift_ref.up_shift_ref) | copy-start | bytes 4612
where the time goes:
time: 52.7 us; the launch traced here: 52.1 us
  Pallas kernels  15.9 us (30%)
  starting transfers between devices  15.3 us (29%)
  local copies, waits for them, and re-layouts  10.6 us (20%)
  waiting for transfers between devices  7.28 us (14%)
  other arithmetic  2.95 us (6%)
    ppermute x11, starting transfers between devices, swapped(): return lax.ppermute(block, axis, [(i, partner(i)) for i in range(n)])  15.3 us
    ppermute x11, waiting for transfers between devices, swapped(): return lax.ppermute(block, axis, [(i, partner(i)) for i in range(n)])  7.28 us
    pallas_call x1, Pallas kernels, inner_of(): pl.pallas_call(inner_kernel, out_shape=jax.ShapeDtypeStruct(shape, BF16),...  5.43 us
    unnamed x26, local copies, waits for them, and re-layouts  5.02 us
    pallas_call x1, Pallas kernels, outer_of(): pl.pallas_call(outer_kernel, out_shape=jax.ShapeDtypeStruct(partial.shape...  4.27 us
    broadcast_in_dim x2, local copies, waits for them, and re-layouts, whole(): fine_gain, fine_shift = (twice(up_gain)[None], twice(up_shift)[None])  2.51 us
    concatenate x3, other arithmetic, whole(): twice = lambda value: jnp.concatenate([value, value], axis=-1)  2.15 us
    pallas_call x1, Pallas kernels, inner_norm(): pl.pallas_call(inner_norm_kernel, out_shape=jax.ShapeDtypeStruct((half_ro...  1.91 us
  transfers between devices with their start and end apart: 11, of which 5 were waited for; matrix products, arithmetic and copies ran while one was open for 16% of the time, Pallas kernels for 19%

commit v1 on v0

--- a/solution.py
+++ b/solution.py
@@ -53,20 +53,30 @@
     return jnp.concatenate([pair[0].astype(F32), pair[1].astype(F32)], axis=-1).astype(BF16)
 
 
+def held(array):
+    return pltpu.with_memory_space_constraint(array, pltpu.HBM)
+
+
 def first_kernel(
-    band_ref, tokens_ref, down_ref, up_ref, shard_ref, core_ref, across_ref, down_s, up_s, rows, sem
+    band_hbm,
+    tokens_ref,
+    down_ref,
+    up_ref,
+    shard_ref,
+    core_ref,
+    across_ref,
+    west_ref,
+    east_ref,
+    tokens_s,
+    band_s,
+    down_s,
+    up_s,
+    sem,
 ):
     tiles, up_tiles = down_ref.shape[0], up_ref.shape[0]
+    slots, columns = tokens_ref.shape[1:3]
     half, features = up_ref.shape[2] // 2, tokens_ref.shape[4]
-    _, live = band(band_ref)
-    even = lax.rem(lax.axis_index("lat"), 2) == 0
-    last = live - 1
-    sources = [
-        (down_ref, down_s),
-        (up_ref, up_s),
-        (tokens_ref.at[:, jnp.where(even, last, 0)], rows.at[0]),
-        (tokens_ref.at[:, jnp.where(even, 0, last)], rows.at[1]),
-    ]
+    sources = [(down_ref, down_s), (up_ref, up_s), (band_hbm, band_s), (tokens_ref, tokens_s)]
     copies = [pltpu.make_async_copy(*pair, sem.at[i]) for i, pair in enumerate(sources)]
     for copy in copies:
         copy.start()
@@ -77,31 +87,43 @@
         ref[:tiles] = down_s[...]
         ref[tiles : tiles + up_tiles] = up[..., :half]
         ref[tiles + up_tiles : tiles + 2 * up_tiles] = up[..., half:]
-    for side, ref in enumerate((core_ref, across_ref)):
-        copies[2 + side].wait()
-        ref[tiles + 2 * up_tiles :] = joined(rows[side])
+    copies[2].wait()
+    odd, live = band(band_s)
+    even = lax.rem(lax.axis_index("lat"), 2) == 0
+    last = live - 1
+    copies[3].wait()
+    for ref, row in ((core_ref, jnp.where(even, last, 0)), (across_ref, jnp.where(even, 0, last))):
+        ref[tiles + 2 * up_tiles :] = joined(tokens_s[:, row])
+    for ref, column in ((west_ref, 0), (east_ref, columns - 1)):
+        ref[pl.ds(odd, slots)] = joined(tokens_s[:, :, column])
 
 
 def first_sends(band_rows, tokens, down, up):
-    members, _, columns, levels, features = tokens.shape
+    members, slots, columns, levels, features = tokens.shape
     tiles, up_tiles = down.shape[0] // 8, up.shape[0] // 8
     n, wide = tiles + 2 * up_tiles, down.shape[1]
     shard = jax.ShapeDtypeStruct((n, 8, wide), BF16)
     with_row = jax.ShapeDtypeStruct((n + columns, 8, wide), BF16)
+    col = jax.ShapeDtypeStruct((slots + 2, levels, members * features), BF16)
     return pl.pallas_call(
         first_kernel,
-        out_shape=(shard, with_row, with_row),
-        in_specs=[SMEM, HBM, HBM, HBM],
-        out_specs=(VMEM,) * 3,
+        out_shape=(shard, with_row, with_row, col, col, jax.ShapeDtypeStruct(tokens.shape, BF16)),
+        in_specs=[HBM] * 4,
+        out_specs=(VMEM,) * 6,
         scratch_shapes=[
+            pltpu.SMEM(band_rows.shape, jnp.int32),
             pltpu.VMEM((tiles, 8, wide), BF16),
             pltpu.VMEM((up_tiles, 8, up.shape[1]), BF16),
-            pltpu.VMEM((2, members, columns, levels, features), BF16),
             pltpu.SemaphoreType.DMA((4,)),
         ],
-        compiler_params=room(2),
+        compiler_params=room(5),
         name="first",
-    )(band_rows, tokens, down.reshape(tiles, 8, -1), up.reshape(up_tiles, 8, -1))
+    )(
+        held(band_rows),
+        held(tokens),
+        held(down.reshape(tiles, 8, -1)),
+        held(up.reshape(up_tiles, 8, -1)),
+    )
 
 
 def rows_kernel(band_ref, tokens_ref, first_ref, last_ref, rows, sem):
@@ -131,7 +153,7 @@
         ],
         compiler_params=room(2),
         name="rows",
-    )(band_rows, tokens)
+    )(band_rows, held(tokens))
 
 
 def edges_kernel(band_ref, tokens_ref, west_ref, east_ref, cols, sem):
@@ -162,42 +184,33 @@
         ],
         compiler_params=room(2),
         name="edges",
-    )(band_rows, tokens)
-
-
-def corners_kernel(band_ref, above_ref, below_ref, west_in, east_in, *out_refs):
+    )(band_rows, held(tokens))
+
+
+def corners_kernel(band_ref, above_ref, below_ref, west_ref, east_ref, near_ref, far_ref):
     odd, live = band(band_ref)
     columns = above_ref.shape[0]
-    west_ref, east_ref, near_ref, far_ref = out_refs
-    west_ref[...] = west_in[...]
-    east_ref[...] = east_in[...]
-    for column, out_ref in ((0, west_ref), (columns - 1, east_ref)):
-        out_ref[pl.ds(live + odd, 1)] = below_ref[pl.ds(column, 1)]
-
-        @pl.when(odd == 1)
+    even = lax.rem(lax.axis_index("lon"), 2) == 0
+    for mine, refs in ((even, (far_ref, near_ref)), (jnp.logical_not(even), (near_ref, far_ref))):
+
+        @pl.when(mine)
         def _():
-            out_ref[pl.ds(0, 1)] = above_ref[pl.ds(column, 1)]
-
-    even = lax.rem(lax.axis_index("lon"), 2) == 0
-
-    @pl.when(even)
-    def _():
-        near_ref[...] = east_ref[...]
-        far_ref[...] = west_ref[...]
-
-    @pl.when(jnp.logical_not(even))
-    def _():
-        near_ref[...] = west_ref[...]
-        far_ref[...] = east_ref[...]
+            for column, in_ref, out_ref in zip((0, columns - 1), (west_ref, east_ref), refs):
+                out_ref[...] = in_ref[...]
+                out_ref[pl.ds(live + odd, 1)] = below_ref[pl.ds(column, 1)]
+
+                @pl.when(odd == 1)
+                def _():
+                    out_ref[pl.ds(0, 1)] = above_ref[pl.ds(column, 1)]
 
 
 def with_corners(band_rows, above, below, west, east):
     out = jax.ShapeDtypeStruct(west.shape, BF16)
     return pl.pallas_call(
         corners_kernel,
-        out_shape=(out,) * 4,
+        out_shape=(out, out),
         in_specs=[SMEM] + [VMEM] * 4,
-        out_specs=(VMEM,) * 4,
+        out_specs=(VMEM,) * 2,
         compiler_params=room(1),
         name="corners",
     )(band_rows, above, below, west, east)
@@ -325,7 +338,7 @@
     return pl.pallas_call(
         inner_norm_kernel,
         out_shape=jax.ShapeDtypeStruct((half_rows // step, rows, 4 * features), BF16),
-        in_specs=[SMEM, HBM] + [VMEM] * 4,
+        in_specs=[SMEM] + [VMEM] * 5,
         out_specs=VMEM,
         scratch_shapes=[
             pltpu.VMEM((members, slots + 2, inner, levels, features), BF16),
@@ -404,9 +417,9 @@
 def outer_kernel(
     band_ref,
     near_ref,
-    west_ref,
-    east_ref,
     far_ref,
+    own_near_ref,
+    own_far_ref,
     gain_ref,
     shift_ref,
     down_ref,
@@ -432,11 +445,8 @@
     for side in range(2):
         parts = []
         for q, p in ORDER:
-            ref = (west_ref, east_ref)[side] if q != side else None
-            if ref is not None:
-                part = rows_at(ref, p)
-            else:
-                part = jnp.where(even == (side == 0), rows_at(far_ref, p), rows_at(near_ref, p))
+            refs = (own_far_ref, own_near_ref) if q != side else (far_ref, near_ref)
+            part = jnp.where(even == (side == 0), *(rows_at(ref, p) for ref in refs))
             parts.append(part)
         averages = member_means(parts[0] + parts[1] + parts[2] + parts[3], lower, 4 * features)
         average = blended(*averages, features - LANES)
@@ -542,7 +552,7 @@
     tiles, up_tiles = down.shape[0] // 8, up.shape[0] // 8
     place = lax.axis_index("lat")
     beside, mirror = lambda i: i ^ 1, lambda i: lat - 1 - i
-    shard, core, across = first_sends(band_rows, tokens, down, up)
+    shard, core, across, west, east, tokens = first_sends(band_rows, tokens, down, up)
     core = swapped(core, "lat", beside)
     across = swapped(across, "lat", mirror)
     z2 = swapped(shard, "lon", lambda i: i ^ 2)
@@ -571,7 +581,7 @@
         name="assemble",
     )(shard, z1, z2, z3, core, across, across12, across3, rest, final)
     down = down.reshape(4, -1, down.shape[-1])
-    return down, up, above, below
+    return down, up, above, below, west, east, tokens
 
 
 def plain_weights(band_rows, tokens, down, up, features):
@@ -585,7 +595,8 @@
     n = down.shape[0]
     up = jnp.stack([whole[:, n : n + rows], whole[:, n + rows :]])
     down = whole[:, :n].reshape(4, features, half)
-    return jnp.pad(down, ((0, 0), (PAD, PAD), (0, 0))), up, above, below
+    down = jnp.pad(down, ((0, 0), (PAD, PAD), (0, 0)))
+    return down, up, above, below, *edges_of(band_rows, tokens), tokens
 
 
 def whole(
@@ -594,26 +605,26 @@
     _, _, _, _, features = tokens.shape
     lon, lat = lax.axis_size("lon"), lax.axis_size("lat")
     block = tokens.transpose(0, 2, 3, 1, 4)
-    west, east = edges_of(band_rows, block)
     plain = lon != 4 or lat != 4 or down_weight.shape[0] % 8 or up_weight.shape[0] % 8
     weights = plain_weights if plain else fast_weights
-    down, up, above, below = weights(band_rows, block, down_weight, up_weight, features)
+    results = weights(band_rows, block, down_weight, up_weight, features)
+    down, up, above, below, west, east, near_by = results
     narrow = down_weight.shape[1]
     up = up.reshape(2, narrow, narrow)
-    west, east, near, far = with_corners(band_rows, above, below, west, east)
-    far = swapped(far, "lon", lambda i: (i - 1 if i % 2 == 0 else i + 1) % lon)
-    near = swapped(near, "lon", lambda i: i ^ 1)
+    own_near, own_far = with_corners(band_rows, above, below, west, east)
+    far = swapped(own_far, "lon", lambda i: (i - 1 if i % 2 == 0 else i + 1) % lon)
+    near = swapped(own_near, "lon", lambda i: i ^ 1)
     gain, shift = down_gain.reshape(4, 1, features), down_shift.reshape(4, 1, features)
     twice = lambda value: jnp.concatenate([value, value], axis=-1)
     fine_gain, fine_shift = twice(up_gain)[None], twice(up_shift)[None]
     mix_weight = jnp.pad(mix_weight, ((PAD, PAD), (0, 0)))
-    normed = inner_norm(band_rows, block, above, below, gain, shift)
+    normed = inner_norm(band_rows, near_by, above, below, gain, shift)
     out = inner_of(
         band_rows, normed, down, up, fine_gain, fine_shift, mix_weight, block.shape
     )
     out = outer_of(
         band_rows,
-        (near, west, east, far),
+        (near, far, own_near, own_far),
         twice(gain),
         twice(shift),
         down,

time: 52.7 us -> 40.8 us (0.77)
  local copies, waits for them, and re-layouts: 10.6 us -> 2.81 us
  other arithmetic: 2.95 us -> 0.27 us
  Pallas kernels: 15.9 us -> 14.2 us
  waiting for transfers between devices: 7.28 us -> 8.04 us
    broadcast_in_dim x2, local copies, waits for them, and re-layouts: 2.51 us -> 0.01 us  [whole(): fine_gain, fine_shift = (twice(up_gain)[None], twice(up_shift)[None])]
    unnamed x26 -> x16, local copies, waits for them, and re-layouts: 5.02 us -> 2.63 us
    concatenate x3, other arithmetic: 2.15 us -> 0.23 us  [whole(): twice = lambda value: jnp.concatenate([value, value], axis=-1)]
    reshape x1, local copies, waits for them, and re-layouts: 1.35 us -> 0.08 us  [whole(): down_shift.reshape(4, 1, features)]
    pad x1, local copies, waits for them, and re-layouts: 0.91 us -> 0.02 us  [whole(): mix_weight = jnp.pad(mix_weight, ((PAD, PAD), (0, 0)))]
    pallas_call x1, Pallas kernels: 1.04 us -> 0.15 us  [fast_weights(): pl.pallas_call(assemble_kernel, out_shape=(jax.ShapeDtypeStruct((lon, lat...]
    pallas_call x3 -> x2, Pallas kernels: 3.17 us -> 2.37 us  [the longest x1 1.76 us: first_sends(): pl.pallas_call(first_kernel, out_shape=(shard, with_row, with_row, col, c...]
    select_n x1, other arithmetic: 0.78 us -> 0.01 us  [fast_weights(): below = jnp.where(place == lat - 1, jnp.zeros_like(below), below)]
  transfers between devices with their start and end apart: 11 -> 11, of which waited for: 5 -> 5; matrix products, arithmetic and copies ran while one was open for 16% -> 1% of each run, Pallas kernels for 19% -> 20%
where the time goes in v1:
time: 40.8 us; the launch traced here: 40.6 us
  starting transfers between devices  15.2 us (37%)
  Pallas kernels  14.2 us (35%)
  waiting for transfers between devices  8.04 us (20%)
  local copies, waits for them, and re-layouts  2.81 us (7%)
    ppermute x11, starting transfers between devices, swapped(): return lax.ppermute(block, axis, [(i, partner(i)) for i in range(n)])  15.2 us
    ppermute x11, waiting for transfers between devices, swapped(): return lax.ppermute(block, axis, [(i, partner(i)) for i in range(n)])  8.04 us
    pallas_call x1, Pallas kernels, inner_of(): pl.pallas_call(inner_kernel, out_shape=jax.ShapeDtypeStruct(shape, BF16),...  5.44 us
    pallas_call x1, Pallas kernels, outer_of(): pl.pallas_call(outer_kernel, out_shape=jax.ShapeDtypeStruct(partial.shape...  4.28 us
    unnamed x16, local copies, waits for them, and re-layouts  2.63 us
    pallas_call x1, Pallas kernels, inner_norm(): pl.pallas_call(inner_norm_kernel, out_shape=jax.ShapeDtypeStruct((half_ro...  1.88 us
    pallas_call x1, Pallas kernels, first_sends(): pl.pallas_call(first_kernel, out_shape=(shard, with_row, with_row, col, c...  1.76 us
  transfers between devices with their start and end apart: 11, of which 5 were waited for; matrix products, arithmetic and copies ran while one was open for 1% of the time, Pallas kernels for 20%

profile of v1, /device:TPU:0, one launch (start us, length us, event | category | flops | bytes accessed | tf_op | source)
XLA Modules:
  0.0 40.6 jit_solution(9865198131875698557)
XLA Ops:
  0.0 0.0 copy-start.6
  0.0 0.0 copy-start.7
  0.0 0.0 copy-start.4
  0.0 0.0 copy-start.5
  0.0 0.0 copy-start
  0.0 1.8 %first.1 = (bf16[12,8,384]{2,1,0:T(8,128)(2,1)S(1)}, bf16[18,8,384]{2,1,0:T(8,128)(2,1)S(1)}, bf16[18,8,384]{2,1,0:T(8,128)(2,1)S(1)}, bf16[36,8,384]{2,1,0:T(8,...) custom-call(s32[1,2]{1,0:T(1,128)} %band_ref.7, ...), custom_call_target="tpu_custom_call" | custom-call | tf_op jit(solution)/shard_map/first/pallas_call | solution.py:108
  1.8 0.0 copy-start.1
  1.8 1.2 %copy-done.1 = bf16[2,34,6,8,192]{4,3,2,1,0:T(8,128)(2,1)} copy-done((bf16[2,34,6,8,192]{4,3,2,1,0:T(8,128)(2,1)}, bf16[2,34,6,8,192]{4,3,2,1,0:T(8,128)(2,1)S(1)}, u32[]{:S(2)}) %copy-start.1) | copy-done | bytes 1253400
  3.0 4.1 %collective-permute-start.5 = (bf16[12,8,384]{2,1,0:T(8,128)(2,1)S(1)}, bf16[12,8,384]{2,1,0:T(8,128)(2,1)S(1)}, u32[]{:S(2)}, u32[]{:S(2)}) collective-permute-start(bf16[12,8,384]{2,1,0:T(8,128)(2,1)S(1)} %get-tuple-element.21.refs_0_), channel_id=1, source_target_pairs={{0,16},{8,24},{16,0},{24,8},{1,17},{9,25},{17,1},{25,9},{2,18},{10... | collective-permute-start | bytes 221192 | tf_op jit(solution)/shard_map/ppermute | solution.py:28
  7.1 1.6 %collective-permute-start.4 = (bf16[12,8,384]{2,1,0:T(8,128)(2,1)S(1)}, bf16[12,8,384]{2,1,0:T(8,128)(2,1)S(1)}, u32[]{:S(2)}, u32[]{:S(2)}) collective-permute-start(bf16[12,8,384]{2,1,0:T(8,128)(2,1)S(1)} %get-tuple-element.21.refs_0_), channel_id=1, source_target_pairs={{0,8},{8,0},{16,24},{24,16},{1,9},{9,1},{17,25},{25,17},{2,10},{10... | collective-permute-start | bytes 221192 | tf_op jit(solution)/shard_map/ppermute | solution.py:28
  8.6 1.8 %collective-permute-done.5.refs_1_.refs_2_ = bf16[12,8,384]{2,1,0:T(8,128)(2,1)S(1)} collective-permute-done((bf16[12,8,384]{2,1,0:T(8,128)(2,1)S(1)}, bf16[12,8,384]{2,1,0:T(8,128)(2,1)S(1)}, u32[]{:S(2)}, u32[]{:S(2)}) %collective-permute-start.5) | collective-permute-done | bytes 73760 | tf_op jit(solution)/shard_map/ppermute | solution.py:28
  10.4 1.0 %collective-permute-done.4.refs_0_.refs_1_ = bf16[12,8,384]{2,1,0:T(8,128)(2,1)S(1)} collective-permute-done((bf16[12,8,384]{2,1,0:T(8,128)(2,1)S(1)}, bf16[12,8,384]{2,1,0:T(8,128)(2,1)S(1)}, u32[]{:S(2)}, u32[]{:S(2)}) %collective-permute-start.4) | collective-permute-done | bytes 73760 | tf_op jit(solution)/shard_map/ppermute | solution.py:28
  11.4 0.6 %collective-permute-start.7 = (bf16[24,8,384]{2,1,0:T(8,128)(2,1)S(1)}, bf16[24,8,384]{2,1,0:T(8,128)(2,1)S(1)}, u32[]{:S(2)}, u32[]{:S(2)}) collective-permute-start(bf16[24,8,384]{2,1,0:T(8,128)(2,1)S(1)} %pad_maximum_fusion), channel_id=1, source_target_pairs={{0,6},{2,4},{4,2},{6,0},{1,7},{3,5},{5,3},{7,1},{8,14},{10,12},{12... | collective-permute-start | bytes 442376 | tf_op jit(solution)/shard_map/ppermute | solution.py:28
  12.1 3.3 %collective-permute-start.6 = (bf16[12,8,384]{2,1,0:T(8,128)(2,1)S(1)}, bf16[12,8,384]{2,1,0:T(8,128)(2,1)S(1)}, u32[]{:S(2)}, u32[]{:S(2)}) collective-permute-start(bf16[12,8,384]{2,1,0:T(8,128)(2,1)S(1)} %get-tuple-element.21.refs_0_), channel_id=1, source_target_pairs={{0,24},{8,16},{16,8},{24,0},{1,25},{9,17},{17,9},{25,1},{2,26},{10... | collective-permute-start | bytes 221192 | tf_op jit(solution)/shard_map/ppermute | solution.py:28
  15.4 0.6 %collective-permute-start = (bf16[18,8,384]{2,1,0:T(8,128)(2,1)S(1)}, bf16[18,8,384]{2,1,0:T(8,128)(2,1)S(1)}, u32[]{:S(2)}, u32[]{:S(2)}) collective-permute-start(bf16[18,8,384]{2,1,0:T(8,128)(2,1)S(1)} %get-tuple-element.15), channel_id=1, source_target_pairs={{0,6},{2,4},{4,2},{6,0},{1,7},{3,5},{5,3},{7,1},{8,14},{10,12},{12... | collective-permute-start | bytes 331784 | tf_op jit(solution)/shard_map/ppermute | solution.py:28
  16.0 0.2 collective-permute-start.1
  16.2 0.0 copy-done.6
  16.2 0.1 pad_maximum_fusion.3
  16.3 2.6 %collective-permute-done.6.refs_2_.refs_3_ = bf16[12,8,384]{2,1,0:T(8,128)(2,1)S(1)} collective-permute-done((bf16[12,8,384]{2,1,0:T(8,128)(2,1)S(1)}, bf16[12,8,384]{2,1,0:T(8,128)(2,1)S(1)}, u32[]{:S(2)}, u32[]{:S(2)}) %collective-permute-start.6) | collective-permute-done | bytes 73760 | tf_op jit(solution)/shard_map/ppermute | solution.py:28
  18.9 1.3 %collective-permute-done.refs_3_.refs_5_ = bf16[18,8,384]{2,1,0:T(8,128)(2,1)S(1)} collective-permute-done((bf16[18,8,384]{2,1,0:T(8,128)(2,1)S(1)}, bf16[18,8,384]{2,1,0:T(8,128)(2,1)S(1)}, u32[]{:S(2)}, u32[]{:S(2)}) %collective-permute-start) | collective-permute-done | bytes 110624 | tf_op jit(solution)/shard_map/ppermute | solution.py:28
  20.1 0.0 collective-permute-done.7.refs_4_.refs_6_
  20.2 0.5 %collective-permute-start.9 = (bf16[72,8,384]{2,1,0:T(8,128)(2,1)S(1)}, bf16[72,8,384]{2,1,0:T(8,128)(2,1)S(1)}, u32[]{:S(2)}, u32[]{:S(2)}) collective-permute-start(bf16[72,8,384]{2,1,0:T(8,128)(2,1)S(1)} %stacked.1), channel_id=1, source_target_pairs={{0,2},{2,0},{4,6},{6,4},{1,3},{3,1},{5,7},{7,5},{8,10},{10,8},{12,... | collective-permute-start | bytes 1327112 | tf_op jit(solution)/shard_map/ppermute | solution.py:28
  20.7 0.0 copy-done.7
  20.7 0.1 pad_maximum_fusion.4
  20.8 0.0 copy-done.4
  20.8 0.1 reshape.20.gain_ref
  20.9 0.0 copy-done.5
  20.9 0.1 reshape.21.shift_ref
  20.9 0.0 copy-done.3
  21.0 0.1 pad_maximum_fusion.1
  21.1 0.6 %collective-permute-start.8 = (bf16[12,8,384]{2,1,0:T(8,128)(2,1)S(1)}, bf16[12,8,384]{2,1,0:T(8,128)(2,1)S(1)}, u32[]{:S(2)}, u32[]{:S(2)}) collective-permute-start(bf16[12,8,384]{2,1,0:T(8,128)(2,1)S(1)} %collective-permute-done.6.refs_2_.refs_3_), channel_id=1, source_target_pairs={{0,6},{2,4},{4,2},{6,0},{1,7},{3,5},{5,3},{7,1},{8,14},{10,12},{12... | collective-permute-start | bytes 221192 | tf_op jit(solution)/shard_map/ppermute | solution.py:28
  21.6 0.0 collective-permute-done.1.refs_4_
  21.7 0.0 copy-done
  21.7 0.6 %corners.1 = (bf16[36,8,384]{2,1,0:T(8,128)(2,1)S(1)}, bf16[36,8,384]{2,1,0:T(8,128)(2,1)S(1)}) custom-call(s32[1,2]{1,0:T(1,128)S(1)} %copy-done, bf16[6,8,384]{2,1,0:T(8,128)(2,1)S(1)} %get-tuple-element.26.above_ref, bf16[6,8,384]{2,1,0:T(8,128)(2,1)S(1)} %get-tuple-element.25.below_ref, bf16[36,8,384]{2,1,0:T(8,128)(2,1)S(1)} %get-tuple-element.17.west_ref, ...), custom_call_target="tpu_custom_call" | custom-call | tf_op jit(solution)/shard_map/corners/pallas_call | solution.py:209
  22.3 1.4 %collective-permute-start.2 = (bf16[36,8,384]{2,1,0:T(8,128)(2,1)S(1)}, bf16[36,8,384]{2,1,0:T(8,128)(2,1)S(1)}, u32[]{:S(2)}, u32[]{:S(2)}) collective-permute-start(bf16[36,8,384]{2,1,0:T(8,128)(2,1)S(1)} %get-tuple-element.19.own_near_ref), channel_id=1, source_target_pairs={{0,8},{8,0},{16,24},{24,16},{1,9},{9,1},{17,25},{25,17},{2,10},{10... | collective-permute-start | bytes 663560 | tf_op jit(solution)/shard_map/ppermute | solution.py:28
  23.7 2.3 %collective-permute-start.3 = (bf16[36,8,384]{2,1,0:T(8,128)(2,1)S(1)}, bf16[36,8,384]{2,1,0:T(8,128)(2,1)S(1)}, u32[]{:S(2)}, u32[]{:S(2)}) collective-permute-start(bf16[36,8,384]{2,1,0:T(8,128)(2,1)S(1)} %get-tuple-element.20.own_far_ref), channel_id=1, source_target_pairs={{0,24},{8,16},{16,8},{24,0},{1,25},{9,17},{17,9},{25,1},{2,26},{10... | collective-permute-start | bytes 663560 | tf_op jit(solution)/shard_map/ppermute | solution.py:28
  25.9 0.0 collective-permute-done.8.refs_7_
  25.9 0.0 collective-permute-start.10
  25.9 0.0 copy-start.2
  26.0 1.4 %copy-done.2 = bf16[2,34,6,8,192]{4,3,2,1,0:T(8,128)(2,1)S(1)} copy-done((bf16[2,34,6,8,192]{4,3,2,1,0:T(8,128)(2,1)S(1)}, bf16[2,34,6,8,192]{4,3,2,1,0:T(8,128)(2,1)}, u32[]{:S(2)}) %copy-start.2) | copy-done | bytes 1253400
  27.4 1.9 %inner_norm.1.normed_ref = bf16[3,192,768]{2,1,0:T(8,128)(2,1)S(1)} custom-call(s32[1,2]{1,0:T(1,128)S(1)} %copy-done, bf16[2,34,6,8,192]{4,3,2,1,0:T(8,128)(2,1)S(1)} %copy-done.2, bf16[6,8,384]{2,1,0:T(8,128)(2,1)S(1)} %get-tuple-element.26.above_ref, bf16[6,8,384]{2,1,0:T(8,128)(2,1)S(1)} %get-tuple-element.25.below_ref, ...), custom_call_target="tpu_custom_call" | custom-call | flops 1000000000 | bytes 1000000 | tf_op jit(solution)/shard_map/inner_norm/pallas_call | solution.py:338
  29.3 0.0 collective-permute-done.10.refs_9_
  29.3 0.0 collective-permute-done.9.refs_8_
  29.3 0.1 assemble.1
  29.5 5.4 %inner.1.partial_ref = bf16[2,34,6,8,192]{4,3,2,1,0:T(8,128)(2,1)} custom-call(s32[1,2]{1,0:T(1,128)S(1)} %copy-done, bf16[3,192,768]{2,1,0:T(8,128)(2,1)S(1)} %inner_norm.1.normed_ref, bf16[4,320,384]{2,1,0:T(8,128)(2,1)S(1)} %bitcast.6, bf16[2,384,384]{2,1,0:T(8,128)(2,1)S(1)} %bitcast.8, f32[1,384]{1,0:T(1,128)S(1)} %broadcast_in_dim.10.gain_ref.up_gain_ref, ...), custom_call_target="tpu_custom_call" | custom-call | flops 4000000000 | bytes 1000000 | tf_op jit(solution)/shard_map/inner/pallas_call | solution.py:385
  34.9 0.0 collective-permute-done.2.near_ref
  34.9 1.4 %collective-permute-done.3.far_ref = bf16[36,8,384]{2,1,0:T(8,128)(2,1)S(1)} collective-permute-done((bf16[36,8,384]{2,1,0:T(8,128)(2,1)S(1)}, bf16[36,8,384]{2,1,0:T(8,128)(2,1)S(1)}, u32[]{:S(2)}, u32[]{:S(2)}) %collective-permute-start.3) | collective-permute-done | bytes 221216 | tf_op jit(solution)/shard_map/ppermute | solution.py:28
  36.4 4.3 %outer.1 = bf16[2,34,6,8,192]{4,3,2,1,0:T(8,128)(2,1)} custom-call(s32[1,2]{1,0:T(1,128)S(1)} %copy-done, bf16[36,8,384]{2,1,0:T(8,128)(2,1)S(1)} %collective-permute-done.2.near_ref, bf16[36,8,384]{2,1,0:T(8,128)(2,1)S(1)} %collective-permute-done.3.far_ref, ...), custom_call_target="tpu_custom_call", output_to_operand_aliasing={{}: (12, {})} | custom-call | flops 3000000000 | bytes 1000000 | tf_op jit(solution)/shard_map/outer/pallas_call | solution.py:493
  (7 shorter events, 0.1 us)
Async XLA Ops:
  0.0 16.2 %copy-start.6 = (f32[192]{0:T(256)S(1)}, f32[192]{0:T(256)}, u32[]{:S(2)}) copy-start(f32[192]{0:T(256)} %param.15) | copy-start | bytes 2308
  0.0 20.7 %copy-start.7 = (f32[192]{0:T(256)S(1)}, f32[192]{0:T(256)}, u32[]{:S(2)}) copy-start(f32[192]{0:T(256)} %param.16) | copy-start | bytes 2308
  0.0 20.8 %copy-start.4 = (f32[768]{0:T(1024)S(1)}, f32[768]{0:T(1024)}, u32[]{:S(2)}) copy-start(f32[768]{0:T(1024)} %param.11) | copy-start | bytes 9220
  0.0 20.9 %copy-start.5 = (f32[768]{0:T(1024)S(1)}, f32[768]{0:T(1024)}, u32[]{:S(2)}) copy-start(f32[768]{0:T(1024)} %param.12) | copy-start | bytes 9220
  0.0 20.9 %copy-start.3 = (bf16[192,192]{1,0:T(8,128)(2,1)S(1)}, bf16[192,192]{1,0:T(8,128)(2,1)}, u32[]{:S(2)}) copy-start(bf16[192,192]{1,0:T(8,128)(2,1)} %param.17) | copy-start | bytes 221188
  0.0 21.7 %copy-start = (s32[1,2]{1,0:T(1,128)S(1)}, s32[1,2]{1,0:T(1,128)}, u32[]{:S(2)}) copy-start(s32[1,2]{1,0:T(1,128)} %band_ref.7) | copy-start | bytes 28
  1.8 1.2 %copy-start.1 = (bf16[2,34,6,8,192]{4,3,2,1,0:T(8,128)(2,1)}, bf16[2,34,6,8,192]{4,3,2,1,0:T(8,128)(2,1)S(1)}, u32[]{:S(2)}) copy-start(bf16[2,34,6,8,192]{4,3,2,1,0:T(8,128)(2,1)S(1)} %get-tuple-element.24.tokens_ref) | copy-start | bytes 3760132
  3.0 7.4 %collective-permute-start.5 = (bf16[12,8,384]{2,1,0:T(8,128)(2,1)S(1)}, bf16[12,8,384]{2,1,0:T(8,128)(2,1)S(1)}, u32[]{:S(2)}, u32[]{:S(2)}) collective-permute-start(bf16[12,8,384]{2,1,0:T(8,128)(2,1)S(1)} %get-tuple-element.21.refs_0_), channel_id=1, source_target_pairs={{0,16},{8,24},{16,0},{24,8},{1,17},{9,25},{17,1},{25,9},{2,18},{10... | collective-permute-start | bytes 221192 | tf_op jit(solution)/shard_map/ppermute | solution.py:28
  7.1 4.4 %collective-permute-start.4 = (bf16[12,8,384]{2,1,0:T(8,128)(2,1)S(1)}, bf16[12,8,384]{2,1,0:T(8,128)(2,1)S(1)}, u32[]{:S(2)}, u32[]{:S(2)}) collective-permute-start(bf16[12,8,384]{2,1,0:T(8,128)(2,1)S(1)} %get-tuple-element.21.refs_0_), channel_id=1, source_target_pairs={{0,8},{8,0},{16,24},{24,16},{1,9},{9,1},{17,25},{25,17},{2,10},{10... | collective-permute-start | bytes 221192 | tf_op jit(solution)/shard_map/ppermute | solution.py:28
  11.4 8.7 %collective-permute-start.7 = (bf16[24,8,384]{2,1,0:T(8,128)(2,1)S(1)}, bf16[24,8,384]{2,1,0:T(8,128)(2,1)S(1)}, u32[]{:S(2)}, u32[]{:S(2)}) collective-permute-start(bf16[24,8,384]{2,1,0:T(8,128)(2,1)S(1)} %pad_maximum_fusion), channel_id=1, source_target_pairs={{0,6},{2,4},{4,2},{6,0},{1,7},{3,5},{5,3},{7,1},{8,14},{10,12},{12... | collective-permute-start | bytes 442376 | tf_op jit(solution)/shard_map/ppermute | solution.py:28
  12.1 6.8 %collective-permute-start.6 = (bf16[12,8,384]{2,1,0:T(8,128)(2,1)S(1)}, bf16[12,8,384]{2,1,0:T(8,128)(2,1)S(1)}, u32[]{:S(2)}, u32[]{:S(2)}) collective-permute-start(bf16[12,8,384]{2,1,0:T(8,128)(2,1)S(1)} %get-tuple-element.21.refs_0_), channel_id=1, source_target_pairs={{0,24},{8,16},{16,8},{24,0},{1,25},{9,17},{17,9},{25,1},{2,26},{10... | collective-permute-start | bytes 221192 | tf_op jit(solution)/shard_map/ppermute | solution.py:28
  15.4 4.7 %collective-permute-start = (bf16[18,8,384]{2,1,0:T(8,128)(2,1)S(1)}, bf16[18,8,384]{2,1,0:T(8,128)(2,1)S(1)}, u32[]{:S(2)}, u32[]{:S(2)}) collective-permute-start(bf16[18,8,384]{2,1,0:T(8,128)(2,1)S(1)} %get-tuple-element.15), channel_id=1, source_target_pairs={{0,6},{2,4},{4,2},{6,0},{1,7},{3,5},{5,3},{7,1},{8,14},{10,12},{12... | collective-permute-start | bytes 331784 | tf_op jit(solution)/shard_map/ppermute | solution.py:28
  16.0 5.6 %collective-permute-start.1 = (bf16[18,8,384]{2,1,0:T(8,128)(2,1)S(1)}, bf16[18,8,384]{2,1,0:T(8,128)(2,1)S(1)}, u32[]{:S(2)}, u32[]{:S(2)}) collective-permute-start(bf16[18,8,384]{2,1,0:T(8,128)(2,1)S(1)} %get-tuple-element.16), channel_id=1, source_target_pairs={{0,2},{2,0},{4,6},{6,4},{1,3},{3,1},{5,7},{7,5},{8,10},{10,8},{12,... | collective-permute-start | bytes 331784 | tf_op jit(solution)/shard_map/ppermute | solution.py:28
  20.2 9.1 %collective-permute-start.9 = (bf16[72,8,384]{2,1,0:T(8,128)(2,1)S(1)}, bf16[72,8,384]{2,1,0:T(8,128)(2,1)S(1)}, u32[]{:S(2)}, u32[]{:S(2)}) collective-permute-start(bf16[72,8,384]{2,1,0:T(8,128)(2,1)S(1)} %stacked.1), channel_id=1, source_target_pairs={{0,2},{2,0},{4,6},{6,4},{1,3},{3,1},{5,7},{7,5},{8,10},{10,8},{12,... | collective-permute-start | bytes 1327112 | tf_op jit(solution)/shard_map/ppermute | solution.py:28
  21.1 4.9 %collective-permute-start.8 = (bf16[12,8,384]{2,1,0:T(8,128)(2,1)S(1)}, bf16[12,8,384]{2,1,0:T(8,128)(2,1)S(1)}, u32[]{:S(2)}, u32[]{:S(2)}) collective-permute-start(bf16[12,8,384]{2,1,0:T(8,128)(2,1)S(1)} %collective-permute-done.6.refs_2_.refs_3_), channel_id=1, source_target_pairs={{0,6},{2,4},{4,2},{6,0},{1,7},{3,5},{5,3},{7,1},{8,14},{10,12},{12... | collective-permute-start | bytes 221192 | tf_op jit(solution)/shard_map/ppermute | solution.py:28
  22.3 12.6 %collective-permute-start.2 = (bf16[36,8,384]{2,1,0:T(8,128)(2,1)S(1)}, bf16[36,8,384]{2,1,0:T(8,128)(2,1)S(1)}, u32[]{:S(2)}, u32[]{:S(2)}) collective-permute-start(bf16[36,8,384]{2,1,0:T(8,128)(2,1)S(1)} %get-tuple-element.19.own_near_ref), channel_id=1, source_target_pairs={{0,8},{8,0},{16,24},{24,16},{1,9},{9,1},{17,25},{25,17},{2,10},{10... | collective-permute-start | bytes 663560 | tf_op jit(solution)/shard_map/ppermute | solution.py:28
  23.7 12.7 %collective-permute-start.3 = (bf16[36,8,384]{2,1,0:T(8,128)(2,1)S(1)}, bf16[36,8,384]{2,1,0:T(8,128)(2,1)S(1)}, u32[]{:S(2)}, u32[]{:S(2)}) collective-permute-start(bf16[36,8,384]{2,1,0:T(8,128)(2,1)S(1)} %get-tuple-element.20.own_far_ref), channel_id=1, source_target_pairs={{0,24},{8,16},{16,8},{24,0},{1,25},{9,17},{17,9},{25,1},{2,26},{10... | collective-permute-start | bytes 663560 | tf_op jit(solution)/shard_map/ppermute | solution.py:28
  25.9 3.3 %collective-permute-start.10 = (bf16[12,8,384]{2,1,0:T(8,128)(2,1)S(1)}, bf16[12,8,384]{2,1,0:T(8,128)(2,1)S(1)}, u32[]{:S(2)}, u32[]{:S(2)}) collective-permute-start(bf16[12,8,384]{2,1,0:T(8,128)(2,1)S(1)} %collective-permute-done.8.refs_7_), channel_id=1, source_target_pairs={{0,2},{2,0},{4,6},{6,4},{1,3},{3,1},{5,7},{7,5},{8,10},{10,8},{12,... | collective-permute-start | bytes 221192 | tf_op jit(solution)/shard_map/ppermute | solution.py:28
  25.9 1.4 %copy-start.2 = (bf16[2,34,6,8,192]{4,3,2,1,0:T(8,128)(2,1)S(1)}, bf16[2,34,6,8,192]{4,3,2,1,0:T(8,128)(2,1)}, u32[]{:S(2)}) copy-start(bf16[2,34,6,8,192]{4,3,2,1,0:T(8,128)(2,1)} %copy-done.1) | copy-start | bytes 3760132
